TPU v7x, 256 devices: a whole 4x4x8 slice. The times are simulated.
256 devices in a mesh: vtx: 64 (over z, y_lo, x), src: 4 (over y_hi, core).
Axes of the slice: x: 4, y: 4 (y_hi: 2, y_lo: 2; y = y_hi * 2 + y_lo), z: 8, core: 2. Of those that a mesh axis runs over, the one named last changes fastest.
Arguments:
- heat: float32 [64, 512, 8192], P(None, ('vtx', 'src')), may hold values from -12 to 12
- cotan: float32 [4, 512, 8192], P(None, 'vtx'), may hold values from 0.2 to 2
- source_index: int32 [64], replicated, may hold values from 0 to 4194303
Outputs:
- normalised: float32 [64, 512, 8192], P('src', 'vtx')
- col_norm: float32 [64], P('src')
Inputs may be any that keep to these rules, and one draw needn't show every extreme that they name: `source_index`: row-major vertex indices, sources may share a vertex.
All inputs are finite; a program needn't handle non-finite values.
Results may differ from a plain program's by a relative error of at most 0.0003.
Values sent between devices are 32-bit elements; how exact they have to be, the bound alone decides.
A program may use at most 64 MiB of HBM per device.

v0:
```python
import math

import jax
import jax.numpy as jnp
from jax import lax
from jax.sharding import PartitionSpec as P


def from_behind(value, axis, by):
    peers = lax.axis_size(axis)
    pairs = [(i, i + by) for i in range(peers) if 0 <= i + by < peers]
    return lax.ppermute(value, axis, pairs)


def extended(value, sides, width):
    for axis, dim in sides:
        peers, length = (lax.axis_size(axis), value.shape[dim])
        up = [(i, (i + 1) % peers) for i in range(peers - 1)]
        down = [(j, i) for i, j in up]
        last = lax.slice_in_dim(value, length - width, length, axis=dim)
        first = lax.slice_in_dim(value, 0, width, axis=dim)
        before = lax.ppermute(last, axis, up)
        after = lax.ppermute(first, axis, down)
        value = jnp.concatenate([before, value, after], axis=dim)
    return value


def from_everyone(value, axis):
    peers = lax.axis_size(axis)
    return lax.all_to_all(
        jnp.broadcast_to(value[None], (peers, *value.shape)), axis, 0, 0, tiled=True
    )


def taken_together(value, axis):
    everything = from_everyone(value, axis)
    return jnp.sum(everything, axis=0)


def from_right(values):
    return jnp.concatenate([values[..., 1:], jnp.zeros_like(values[..., :1])], axis=-1)


def from_left(values):
    return jnp.concatenate([jnp.zeros_like(values[..., :1]), values[..., :-1]], axis=-1)


def masked_cotan(cotan, row_start, total_rows):
    shape = cotan.shape[1:]
    rows = row_start + lax.broadcasted_iota(jnp.int32, shape, 0)
    cols = lax.broadcasted_iota(jnp.int32, shape, 1)
    inside_col = cols < shape[1] - 1
    inside_row = rows < total_rows - 1
    mass = cotan[0]
    east = jnp.where(inside_col, cotan[1], 0.0)
    north = jnp.where(inside_row, cotan[2], 0.0)
    diag = jnp.where(inside_col & inside_row, cotan[3], 0.0)
    return (mass, east, north, diag)


def stencil_defect(padded, mass, east, north_ext, diag_ext, row_start, sources, amplitude):
    center = padded[:, 1:-1, :]
    above = padded[:, 2:, :]
    below = padded[:, :-2, :]
    north = north_ext[1:]
    south_weight = north_ext[:-1]
    diag = diag_ext[1:]
    southwest_weight = from_left(diag_ext[:-1])
    west_weight = from_left(east)
    result = mass * center + east * (center - from_right(center))
    result = result + west_weight * (center - from_left(center))
    result = result + north * (center - above) + south_weight * (center - below)
    result = (
        result
        + diag * (center - from_right(above))
        + southwest_weight * (center - from_left(below))
    )
    count_rows, width = (center.shape[1], center.shape[2])
    row_ids = row_start + lax.broadcasted_iota(jnp.int32, (count_rows, width), 0)
    col_ids = lax.broadcasted_iota(jnp.int32, (count_rows, width), 1)
    flat = row_ids * width + col_ids
    delta = (flat[None, :, :] == sources[:, None, None]).astype(jnp.float32)
    return result - amplitude * delta


def on_device(heat, cotan, source_index):
    vtx_index = lax.axis_index("vtx")
    rows_dev = cotan.shape[1]
    width = cotan.shape[2]
    total_rows = rows_dev * lax.axis_size("vtx")
    amplitude = math.sqrt(total_rows * width) / 8.0
    block_start = vtx_index * rows_dev
    mass, east, north, diag = masked_cotan(cotan, block_start, total_rows)
    lower = from_behind(jnp.stack([north[-1:], diag[-1:]]), "vtx", 1)
    north_ext = jnp.concatenate([lower[0], north], axis=0)
    diag_ext = jnp.concatenate([lower[1], diag], axis=0)
    src_index = lax.axis_index("src")
    per_group = heat.shape[0] // lax.axis_size("src")
    tile = lax.all_to_all(heat, "src", split_axis=0, concat_axis=1, tiled=True)
    padded = extended(tile, (("vtx", 1),), 1)
    sources = lax.dynamic_slice_in_dim(source_index, src_index * per_group, per_group)
    defect = stencil_defect(
        padded, mass, east, north_ext, diag_ext, block_start, sources, amplitude
    )
    total = taken_together(jnp.sum(defect * defect, axis=(1, 2)), "vtx")
    norms = jnp.sqrt(total / (total_rows * width) + 1e-06)
    return (defect / norms[:, None, None], norms)


def solution(mesh):
    return jax.shard_map(
        on_device,
        mesh=mesh,
        in_specs=(P(None, ("vtx", "src"), None), P(None, "vtx", None), P()),
        out_specs=(P("src", "vtx", None), P("src")),
        check_vma=False,
    )
```

profile of v0, /device:TPU:1, one launch (start us, length us, event | category | flops | bytes accessed | tf_op | source)
XLA Modules:
  0.0 117.2 jit_solution(17329714812238578994)
XLA Ops:
  0.6 0.0 copy-start
  0.6 8.1 %all-to-all-start = ((f32[64,2,8192]{2,1,0:T(2,128)}), f32[64,2,8192]{2,1,0:T(2,128)}, u32[]{:S(2)}, u32[]{:S(2)}) async-start(f32[64,2,8192]{2,1,0:T(2,128)} %param.3), calls=%async_computation | async-start | bytes 8388608 | tf_op jit(solution)/shard_map/all_to_all | solution.py:99
  8.8 0.1 bitcast_select_fusion.1
  9.0 0.1 pad_maximum_fusion.1
  9.1 1.4 %collective-permute-start.1 = (f32[2,1,8192]{2,1,0:T(1,128)S(1)}, f32[2,1,8192]{2,1,0:T(1,128)S(1)}, u32[]{:S(2)}, u32[]{:S(2)}) collective-permute-start(f32[2,1,8192]{2,1,0:T(1,128)S(1)} %pad_maximum_fusion.1), channel_id=1, source_target_pairs={{0,4},{4,8},{8,12},{12,16},{16,20},{20,24},{24,28},{28,32},{32,36}... | collective-permute-start | bytes 196616 | tf_op jit(solution)/shard_map/ppermute | solution.py:12
  10.5 0.1 slice_bitcast_fusion
  10.7 0.1 iota_add_fusion
  10.8 0.1 dynamic_slice.3
  10.9 0.1 concatenate.32
  11.0 0.8 collective-permute-done.1
  11.8 0.2 select_maximum_fusion.2
  12.0 46.9 %all-to-all-done = f32[64,2,8192]{2,1,0:T(2,128)} async-done(((f32[64,2,8192]{2,1,0:T(2,128)}), f32[64,2,8192]{2,1,0:T(2,128)}, u32[]{:S(2)}, u32[]{:S(2)}) %all-to-all-start) | async-done | bytes 4194336 | tf_op jit(solution)/shard_map/all_to_all | solution.py:99
  59.0 4.6 %copy.10 = f32[4,16,2,8192]{3,1,2,0:T(8,128)S(1)} copy(f32[4,16,2,8192]{3,2,1,0:T(2,128)} %bitcast.1) | data formatting | bytes 8388608 | tf_op jit(solution)/shard_map/all_to_all | solution.py:99
  63.6 0.1 fusion.19
  63.7 1.3 %collective-permute-start = (f32[16,1,8192]{2,0,1:T(8,128)S(1)}, f32[16,1,8192]{2,0,1:T(8,128)S(1)}, u32[]{:S(2)}, u32[]{:S(2)}) collective-permute-start(f32[16,1,8192]{2,0,1:T(8,128)S(1)} %get-tuple-element.12), channel_id=1, source_target_pairs={{4,0},{8,4},{12,8},{16,12},{20,16},{24,20},{28,24},{32,28},{36,32}... | collective-permute-start | bytes 1572872 | tf_op jit(solution)/shard_map/ppermute | solution.py:23
  65.0 4.0 %collective-permute-start.2 = (f32[16,1,8192]{2,0,1:T(8,128)S(1)}, f32[16,1,8192]{2,0,1:T(8,128)S(1)}, u32[]{:S(2)}, u32[]{:S(2)}) collective-permute-start(f32[16,1,8192]{2,0,1:T(8,128)S(1)} %get-tuple-element.13), channel_id=1, source_target_pairs={{0,4},{4,8},{8,12},{12,16},{16,20},{20,24},{24,28},{28,32},{32,36}... | collective-permute-start | bytes 1572872 | tf_op jit(solution)/shard_map/ppermute | solution.py:22
  69.0 1.5 %fusion.18 = (f32[16,8,8191]{2,0,1:T(8,128)S(1)}, f32[16,8,8191]{2,0,1:T(8,128)S(1)}) fusion(f32[16,8,8192]{2,0,1:T(8,128)S(1)} %bitcast.28), kind=kLoop, calls=%fused_computation.47 | loop fusion | bytes 16775168 | tf_op jit(solution)/shard_map/slice | solution.py:41
  70.5 7.6 %collective-permute-done = f32[16,1,8192]{2,0,1:T(8,128)S(1)} collective-permute-done((f32[16,1,8192]{2,0,1:T(8,128)S(1)}, f32[16,1,8192]{2,0,1:T(8,128)S(1)}, u32[]{:S(2)}, u32[]{:S(2)}) %collective-permute-start) | collective-permute-done | bytes 524320 | tf_op jit(solution)/shard_map/ppermute | solution.py:23
  78.1 0.9 collective-permute-done.2
  79.0 7.7 %multiply_reduce_fusion = (f32[16]{0:T(128)S(1)}, f32[16,8,8192]{2,0,1:T(8,128)}) fusion(s32[16]{0:T(128)S(1)} %dynamic_slice.3, s32[8,8192]{1,0:T(8,128)S(1)} %iota_add_fusion, f32[16,8,8192]{2,0,1:T(8,128)S(1)} %bitcast.29, f32[16,1,8192]{2,0,1:T(8,128)S(1)} %collective-permute-done.2, f32[8,8192]{1,0:T(8,128)S(1)} %get-tuple-element.26, ...), kind=kLoop, calls=%fused_computation.23 | loop fusion | flops 35651568 | bytes 19922048 | tf_op jit(solution)/shard_map/reduce_sum | solution.py:105
  86.7 23.2 %all_to_all.24 = f32[64,1,16]{2,1,0:T(1,128)S(1)} all-to-all(f32[64,1,16]{2,1,0:T(1,128)S(1)} %broadcast_in_dim.12), channel_id=1, replica_groups=mesh['vtx'=64,'src'=4] {'vtx'}, dimensions={0} | all-to-all | bytes 8192 | tf_op jit(solution)/shard_map/all_to_all | solution.py:30
  109.9 0.1 reduce_sum.19
  110.0 2.7 %broadcast_divide_fusion = f32[16,8,8192]{2,0,1:T(8,128)S(1)} fusion(f32[16,8,8192]{2,0,1:T(8,128)} %get-tuple-element.9, f32[16]{0:T(128)S(1)} %add_sqrt_fusion), kind=kLoop, calls=%fused_computation.24 | loop fusion | flops 1048576 | bytes 8388672 | tf_op jit(solution)/shard_map/div | solution.py:107
  112.7 4.4 %copy.12 = f32[16,8,8192]{2,1,0:T(8,128)} copy(f32[16,8,8192]{2,0,1:T(8,128)S(1)} %broadcast_divide_fusion) | data formatting | bytes 8388608
  (14 shorter events, 0.2 us)
Async XLA Ops:
  0.6 8.2 %copy-start = (f32[4,8,8192]{2,1,0:T(8,128)S(1)}, f32[4,8,8192]{2,1,0:T(8,128)}, u32[]{:S(2)}) copy-start(f32[4,8,8192]{2,1,0:T(8,128)} %param.4) | copy-start | bytes 3145732
  0.6 58.3 %all-to-all-start = ((f32[64,2,8192]{2,1,0:T(2,128)}), f32[64,2,8192]{2,1,0:T(2,128)}, u32[]{:S(2)}, u32[]{:S(2)}) async-start(f32[64,2,8192]{2,1,0:T(2,128)} %param.3), calls=%async_computation | async-start | bytes 8388608 | tf_op jit(solution)/shard_map/all_to_all | solution.py:99
  8.8 2.0 %copy-start.2 = (s32[64]{0:T(128)S(1)}, s32[64]{0:T(128)}, u32[]{:S(2)}) copy-start(s32[64]{0:T(128)} %param.5) | copy-start | bytes 772
  9.1 2.7 %collective-permute-start.1 = (f32[2,1,8192]{2,1,0:T(1,128)S(1)}, f32[2,1,8192]{2,1,0:T(1,128)S(1)}, u32[]{:S(2)}, u32[]{:S(2)}) collective-permute-start(f32[2,1,8192]{2,1,0:T(1,128)S(1)} %pad_maximum_fusion.1), channel_id=1, source_target_pairs={{0,4},{4,8},{8,12},{12,16},{16,20},{20,24},{24,28},{28,32},{32,36}... | collective-permute-start | bytes 196616 | tf_op jit(solution)/shard_map/ppermute | solution.py:12
  63.7 14.4 %collective-permute-start = (f32[16,1,8192]{2,0,1:T(8,128)S(1)}, f32[16,1,8192]{2,0,1:T(8,128)S(1)}, u32[]{:S(2)}, u32[]{:S(2)}) collective-permute-start(f32[16,1,8192]{2,0,1:T(8,128)S(1)} %get-tuple-element.12), channel_id=1, source_target_pairs={{4,0},{8,4},{12,8},{16,12},{20,16},{24,20},{28,24},{32,28},{36,32}... | collective-permute-start | bytes 1572872 | tf_op jit(solution)/shard_map/ppermute | solution.py:23
  65.0 14.0 %collective-permute-start.2 = (f32[16,1,8192]{2,0,1:T(8,128)S(1)}, f32[16,1,8192]{2,0,1:T(8,128)S(1)}, u32[]{:S(2)}, u32[]{:S(2)}) collective-permute-start(f32[16,1,8192]{2,0,1:T(8,128)S(1)} %get-tuple-element.13), channel_id=1, source_target_pairs={{0,4},{4,8},{8,12},{12,16},{16,20},{20,24},{24,28},{28,32},{32,36}... | collective-permute-start | bytes 1572872 | tf_op jit(solution)/shard_map/ppermute | solution.py:22
  110.0 2.7 %copy-start.1 = (f32[16]{0:T(128)}, f32[16]{0:T(128)S(1)}, u32[]{:S(2)}) copy-start(f32[16]{0:T(128)S(1)} %add_sqrt_fusion) | copy-start | bytes 196
where the time goes:
time: 119 us; the launch traced here: 117 us
  waiting for transfers between devices  56.3 us (47%)
  blocking collectives  23.2 us (19%)
  starting transfers between devices  14.9 us (13%)
  other arithmetic  11.2 us (9%)
  local copies, waits for them, and re-layouts  10.9 us (9%)
    all_to_all x1, waiting for transfers between devices, on_device(): tile = lax.all_to_all(heat, 'src', split_axis=0, concat_axis=1, tiled=True)  46.9 us
    all_to_all x1, blocking collectives, from_everyone(): lax.all_to_all(jnp.broadcast_to(value[None], (peers, *value.shape)), axis...  23.2 us
    all_to_all x1, starting transfers between devices, on_device(): tile = lax.all_to_all(heat, 'src', split_axis=0, concat_axis=1, tiled=True)  8.13 us
    reduce_sum x1, other arithmetic, on_device(): total = taken_together(jnp.sum(defect * defect, axis=(1, 2)), 'vtx')  7.69 us
    ppermute x1, waiting for transfers between devices, extended(): after = lax.ppermute(first, axis, down)  7.61 us
    all_to_all x1, local copies, waits for them, and re-layouts, on_device(): tile = lax.all_to_all(heat, 'src', split_axis=0, concat_axis=1, tiled=True)  4.62 us
    unnamed x7, local copies, waits for them, and re-layouts  4.45 us
    ppermute x1, starting transfers between devices, extended(): before = lax.ppermute(last, axis, up)  4.02 us
  transfers between devices with their start and end apart: 4, of which 4 were waited for; matrix products, arithmetic and copies ran while one was open for 2% of the time, Pallas kernels for 0%

commit v1 on v0

v1 whole, which is shorter than its diff:
```python
import functools
import math

import jax
import jax.numpy as jnp
from jax import lax
from jax.experimental import pallas as pl
from jax.experimental.pallas import tpu as pltpu
from jax.sharding import PartitionSpec as P

MESH = pl.DeviceIdType.MESH
RING = 4
PLANE = 8
GROUP = 2
LANES = 128
F32 = jnp.float32
ABOVE, BELOW = 8, 15


def at(v, k):
    return {"vtx": v, "src": k}


def remote(src, dst, send, recv, target):
    return pltpu.make_async_remote_copy(
        src_ref=src,
        dst_ref=dst,
        send_sem=send,
        recv_sem=recv,
        device_id=target,
        device_id_type=MESH,
    )


def signal(sem, target):
    pl.semaphore_signal(sem, inc=1, device_id=target, device_id_type=MESH)


def each(count, body):
    lax.fori_loop(0, count, lambda i, _: (body(i), 0)[1], 0)


def shifted_weights(cot, lower, weights, v, total_rows, width):
    tiles = width // LANES
    lane = lax.broadcasted_iota(jnp.int32, (8, LANES), 1)
    sub = lax.broadcasted_iota(jnp.int32, (8, LANES), 0)
    in_row = sub + 8 * v < total_rows - 1
    has_lower = jnp.full((8, LANES), v, jnp.int32) > 0

    def tile(j):
        cols = pl.ds(pl.multiple_of(j * LANES, LANES), LANES)
        in_col = lane + j * LANES < width - 1
        east = jnp.where(in_col, cot[1, :, cols], 0.0)
        north = jnp.where(in_row, cot[2, :, cols], 0.0)
        diag = jnp.where(in_col & in_row, cot[3, :, cols], 0.0)
        low_n = jnp.where(has_lower, lower[0, :, cols], 0.0)
        low_d = jnp.where(has_lower & in_col, lower[1, :, cols], 0.0)
        south = jnp.where(sub == 0, low_n, pltpu.roll(north, 1, 0))
        diag_s = jnp.where(sub == 0, low_d, pltpu.roll(diag, 1, 0))
        return cols, east, north, diag, south, diag_s

    def body(j):
        cols, east, north, diag, south, diag_s = tile(j)
        _, east_l, _, diag_l, _, diag_sl = tile(lax.rem(j + tiles - 1, tiles))

        def right(here, left):
            return jnp.where(lane == 0, pltpu.roll(left, 1, 1), pltpu.roll(here, 1, 1))

        west = right(east, east_l)
        diag_w = right(diag, diag_l)
        southwest = right(diag_s, diag_sl)
        weights[0, :, cols] = (
            cot[0, :, cols] + east + west + north + south + diag + southwest
        )
        weights[1, :, cols] = north
        weights[2, :, cols] = south
        weights[3, :, cols] = east
        weights[4, :, cols] = west
        weights[5, :, cols] = diag_w
        weights[6, :, cols] = diag_s

    each(tiles, body)


def field_defect(field, weights, out, s, where, amplitude, width):
    lane = lax.broadcasted_iota(jnp.int32, (8, LANES), 1)
    sub = lax.broadcasted_iota(jnp.int32, (8, LANES), 0)
    flat = sub * width + lane
    step = 8

    def block(b, carry):
        partial, east_at, west_at, acc, rel = carry
        for i in range(step):
            j = b * step + i
            cols = pl.ds(pl.multiple_of(j * LANES, LANES), LANES)
            h = field[s, 0:8, cols]
            halo = field[s, 8:16, cols]
            above = pltpu.roll(jnp.where(sub == 0, halo, h), 7, 0)
            below = pltpu.roll(jnp.where(sub == 7, halo, h), 1, 0)
            to_left = weights[4, :, cols] * h + weights[5, :, cols] * above
            to_right = weights[3, :, cols] * h + weights[6, :, cols] * below
            to_left = pltpu.roll(to_left, LANES - 1, 1)
            to_right = pltpu.roll(to_right, 1, 1)
            done = partial - jnp.where(lane == LANES - 1, to_left, east_at)
            before = pl.ds(
                pl.multiple_of(jnp.maximum(j - 1, 0) * LANES, LANES), LANES
            )
            out[s, :, before] = done
            if i == 0:
                acc = jnp.where(jnp.full((8, LANES), b) > 0, acc + done * done, acc)
            else:
                acc = acc + done * done
            partial = (
                weights[0, :, cols] * h
                - weights[1, :, cols] * above
                - weights[2, :, cols] * below
                - jnp.where(lane == 0, west_at, to_right)
                - jnp.where(flat == rel, amplitude, 0.0)
            )
            east_at, west_at = to_left, to_right
            rel = rel - LANES
        return partial, east_at, west_at, acc, rel

    zero = jnp.zeros((8, LANES), F32)
    rel = jnp.full((8, LANES), where, jnp.int32)
    partial, east_at, _, acc, _ = lax.fori_loop(
        0, width // LANES // step, block, (zero, zero, zero, zero, rel)
    )
    done = partial - jnp.where(lane == LANES - 1, 0.0, east_at)
    out[s, :, width - LANES :] = done
    return acc + done * done


def kernel(
    peers,
    amplitude,
    heat,
    cot_hbm,
    cot,
    sources,
    out,
    norms,
    field,
    lower,
    weights,
    relay,
    row,
    rows,
    own_sem,
    low_send,
    low_recv,
    send,
    recv,
    halo_send,
    halo_recv,
    edge_send,
    relay_send,
    relay_recv,
    sum_send,
    sum_recv,
):
    v, k = lax.axis_index("vtx"), lax.axis_index("src")
    x = lax.rem(v, RING)
    width = field.shape[2]
    per = field.shape[0]
    chunks = per // GROUP
    up, down = lax.rem(v + 1, peers), lax.rem(v + peers - 1, peers)
    line = v - x
    plane = v - lax.rem(v, PLANE)
    top, bottom = k == 3, k == 0
    last, first = x == RING - 1, x == 0

    def in_plane(i):
        inside = lax.rem(v, PLANE)
        return (
            plane
            + lax.rem(inside // RING + i // RING, PLANE // RING) * RING
            + lax.rem(inside + i, RING)
        )

    def in_depth(i):
        return lax.rem(v + PLANE * i, peers)

    depth = peers // PLANE
    barrier = pltpu.get_barrier_semaphore()
    for q in (1, 2, 3):
        signal(barrier, at(v, k ^ q))
    for q in (0, 1):
        signal(barrier, at(up, k ^ q))
        signal(barrier, at(down, k ^ q))
    for i in range(1, PLANE):
        signal(barrier, at(in_plane(i), k))
    for i in range(1, depth):
        signal(barrier, at(in_depth(i), k))
    signal(barrier, at(lax.rem(line + peers - 1, peers), 3))
    signal(barrier, at(lax.rem(line + RING, peers), 0))
    known = 7 + (PLANE - 1) + (depth - 1)
    wraps = (top & last) | (bottom & first)

    @pl.when(wraps)
    def _():
        pl.semaphore_wait(barrier, known + 4 * RING)

    @pl.when(jnp.logical_not(wraps))
    def _():
        pl.semaphore_wait(barrier, known)

    own = pltpu.make_async_copy(
        heat.at[pl.ds(per * k, per)],
        field.at[:, pl.ds(pl.multiple_of(2 * k, 2), 2)],
        own_sem,
    )
    own.start()
    low = remote(
        cot_hbm.at[pl.ds(2, 2), 7], lower.at[:, 0], low_send, low_recv, at(up, k)
    )
    low.start()

    def some(c):
        return pl.ds(c * GROUP, GROUP)

    def edge_copies(c, act):
        for m in range(4):
            data = heat.at[pl.ds(per * m + c * GROUP, GROUP)]
            via = lax.rem(c, RING)
            slot = c // RING

            @pl.when(top & last & (via == 0))
            def _():
                act(
                    remote(
                        data.at[:, 1],
                        field.at[some(c), BELOW],
                        edge_send.at[c, m],
                        halo_recv.at[c, 0],
                        at(up, m),
                    )
                )

            @pl.when(top & last & (via != 0))
            def _():
                act(
                    remote(
                        data.at[:, 1],
                        relay.at[0, slot],
                        edge_send.at[c, m],
                        relay_recv.at[0, slot],
                        at(up + via, m),
                    )
                )

            @pl.when(bottom & first & (via == RING - 1))
            def _():
                act(
                    remote(
                        data.at[:, 0],
                        field.at[some(c), ABOVE],
                        edge_send.at[c, m],
                        halo_recv.at[c, 1],
                        at(down, m),
                    )
                )

            @pl.when(bottom & first & (via != RING - 1))
            def _():
                act(
                    remote(
                        data.at[:, 0],
                        relay.at[1, slot],
                        edge_send.at[c, m],
                        relay_recv.at[1, slot],
                        at(down - (RING - 1) + via, m),
                    )
                )

            if m >= 2:

                @pl.when(top & jnp.logical_not(last))
                def _():
                    act(
                        remote(
                            data.at[:, 1],
                            field.at[some(c), BELOW],
                            edge_send.at[c, m],
                            halo_recv.at[c, 0],
                            at(up, m),
                        )
                    )
            else:

                @pl.when(bottom & jnp.logical_not(first))
                def _():
                    act(
                        remote(
                            data.at[:, 0],
                            field.at[some(c), ABOVE],
                            edge_send.at[c, m],
                            halo_recv.at[c, 1],
                            at(down, m),
                        )
                    )

    start = lambda d: d.start()
    wait_send = lambda d: d.wait_send()
    wait_recv = lambda d: d.wait_recv()

    edge_row = jnp.where(top, 1, 0)

    def exchange(c, i, q, phase):
        to = k ^ q
        r = edge_row if phase == 0 else 1 - edge_row
        return remote(
            heat.at[pl.ds(per * to + c * GROUP, GROUP), r],
            field.at[some(c), 2 * k + r],
            send.at[c, i, phase],
            recv.at[c, i, phase],
            at(v, to),
        )

    def begin(c):
        exchange(c, 0, 2, 0).start()
        exchange(c, 1, 3, 0).start()
        edge_copies(c, start)

    each(chunks, begin)

    def begin_rest(c):
        exchange(c, 2, 1, 0).start()
        exchange(c, 2, 1, 1).start()
        exchange(c, 0, 2, 1).start()
        exchange(c, 1, 3, 1).start()

    each(chunks, begin_rest)

    low.wait_recv()
    shifted_weights(cot, lower, weights, v, peers * 8, width)

    came = jnp.where((k == 0) | (k == 3), 1, 0)
    inner_up = (k < 2) & jnp.logical_not(last)
    inner_down = (k >= 2) & jnp.logical_not(first)

    def forward(c, act):
        @pl.when(inner_up)
        def _():
            act(
                remote(
                    field.at[some(c), 7],
                    field.at[some(c), BELOW],
                    halo_send.at[c],
                    halo_recv.at[c, 0],
                    at(up, k),
                )
            )

        @pl.when(inner_down)
        def _():
            act(
                remote(
                    field.at[some(c), 0],
                    field.at[some(c), ABOVE],
                    halo_send.at[c],
                    halo_recv.at[c, 1],
                    at(down, k),
                )
            )

    def relayed(slot, act):
        c = x + RING * slot

        @pl.when(jnp.logical_not(first))
        def _():
            act(
                remote(
                    relay.at[0, slot],
                    field.at[some(c), BELOW],
                    relay_send.at[0, slot],
                    halo_recv.at[c, 0],
                    at(line, k),
                ),
                0,
                slot,
            )

        @pl.when(jnp.logical_not(last))
        def _():
            act(
                remote(
                    relay.at[1, slot],
                    field.at[some(c), ABOVE],
                    relay_send.at[1, slot],
                    halo_recv.at[c, 1],
                    at(line + RING - 1, k),
                ),
                1,
                slot,
            )

    def relay_on(copy, side, slot):
        arrived(relay.at[side, slot], relay_recv.at[side, slot])
        copy.start()

    def arrived(ref, sem):
        pltpu.make_async_copy(ref, ref, sem).wait()

    def pass_on(c):
        arrived(field.at[some(c), 0], recv.at[c, came, 0])
        forward(c, start)

    for slot in range(chunks // RING):
        for c in range(slot * RING, (slot + 1) * RING):
            pass_on(c)
        relayed(slot, relay_on)

    own.wait()
    lane = lax.broadcasted_iota(jnp.int32, (1, LANES), 1)
    base = v * (8 * width)

    def chunk(c, sums):
        arrived(field.at[some(c), 0], recv.at[c, 1 - came, 0])
        arrived(field.at[some(c), 0], recv.at[c, 2, 0])
        for i in range(3):
            arrived(field.at[some(c), 0], recv.at[c, i, 1])
        for i in range(2):
            arrived(field.at[some(c), 0], halo_recv.at[c, i])

        def one(g, sums):
            s = c * GROUP + g
            acc = field_defect(
                field, weights, out, s, sources[per * k + s] - base, amplitude, width
            )
            total = jnp.sum(acc, axis=(0, 1), keepdims=True)
            return sums + jnp.where(lane == s, total, 0.0)

        return lax.fori_loop(0, GROUP, one, sums)

    sums = lax.fori_loop(0, chunks, chunk, jnp.zeros((1, LANES), F32))

    def exchanged(which, value, count, place, back):
        row[which] = value
        copies = []
        for i in range(1, count):
            copies.append(
                remote(
                    row.at[which],
                    rows.at[which, back(i)],
                    sum_send.at[which, i],
                    sum_recv.at[which, back(i)],
                    at(place(i), k),
                )
            )
            copies[-1].start()
        for i in range(1, count):
            arrived(row.at[which], sum_recv.at[which, i])
            value = value + rows[which, i]
        return value, copies

    sums, sent = exchanged(
        0,
        sums,
        PLANE,
        in_plane,
        lambda i: (i // RING) * RING + (RING - i % RING) % RING,
    )
    sums, more = exchanged(1, sums, depth, in_depth, lambda i: depth - i)
    norms[...] = jnp.sqrt(sums / (peers * 8 * width) + 1e-06)

    for copy in sent + more:
        copy.wait_send()
    low.wait_send()

    def left(c):
        for phase in range(2):
            exchange(c, 0, 2, phase).wait_send()
            exchange(c, 1, 3, phase).wait_send()
            exchange(c, 2, 1, phase).wait_send()
        edge_copies(c, wait_send)
        forward(c, wait_send)

    each(chunks, left)
    for slot in range(chunks // RING):
        relayed(slot, lambda copy, side, slot: copy.wait_send())


def on_device(heat, cotan, source_index):
    peers = lax.axis_size("vtx")
    rows_dev, width = cotan.shape[1:]
    per = heat.shape[0] // lax.axis_size("src")
    chunks = per // GROUP
    amplitude = math.sqrt(rows_dev * peers * width) / 8.0
    dma, vmem = pltpu.SemaphoreType.DMA, pltpu.VMEM
    anywhere = pl.BlockSpec(memory_space=pl.ANY)
    held = pl.BlockSpec(memory_space=pltpu.VMEM)
    defect, norms = pl.pallas_call(
        functools.partial(kernel, peers, amplitude),
        name="defect",
        out_shape=(
            jax.ShapeDtypeStruct((per, rows_dev, width), F32),
            jax.ShapeDtypeStruct((1, LANES), F32),
        ),
        in_specs=[
            anywhere,
            anywhere,
            held,
            pl.BlockSpec(memory_space=pltpu.SMEM),
        ],
        out_specs=(held, held),
        scratch_shapes=[
            vmem((per, 2 * rows_dev, width), F32),
            vmem((2, 8, width), F32),
            vmem((7, rows_dev, width), F32),
            vmem((2, chunks // RING, GROUP, width), F32),
            vmem((2, 1, LANES), F32),
            vmem((2, PLANE, 1, LANES), F32),
            dma,
            dma,
            dma,
            dma((chunks, 3, 2)),
            dma((chunks, 3, 2)),
            dma((chunks,)),
            dma((chunks, 2)),
            dma((chunks, 4)),
            dma((2, chunks // RING)),
            dma((2, chunks // RING)),
            dma((2, PLANE)),
            dma((2, PLANE)),
        ],
        compiler_params=pltpu.CompilerParams(
            collective_id=0, has_side_effects=True, vmem_limit_bytes=40 << 20
        ),
        cost_estimate=pl.CostEstimate(
            flops=200_000_000, bytes_accessed=16_000_000, transcendentals=0
        ),
    )(heat, cotan, cotan, source_index)
    norms = norms[0, :per]
    return (defect / norms[:, None, None], norms)


def solution(mesh):
    return jax.shard_map(
        on_device,
        mesh=mesh,
        in_specs=(P(None, ("vtx", "src"), None), P(None, "vtx", None), P()),
        out_specs=(P("src", "vtx", None), P("src")),
        check_vma=False,
    )
```

time: 119 us -> 81.7 us (0.69); the launches traced: 117 us -> 81.4 us
  Pallas kernels: 0 us -> 74.2 us
  waiting for transfers between devices: 56.3 us -> 0 us
  blocking collectives: 23.2 us -> 0 us
  starting transfers between devices: 14.9 us -> 0 us
  other arithmetic: 11.2 us -> 2.48 us
  local copies, waits for them, and re-layouts: 10.9 us -> 4.07 us
    pallas_call x0 -> x1, Pallas kernels: none -> 74.2 us  [on_device(): pl.pallas_call(functools.partial(kernel, peers, amplitude), name='defect'...]
    all_to_all x1 -> x0, waiting for transfers between devices: 46.9 us -> none  [on_device(): tile = lax.all_to_all(heat, 'src', split_axis=0, concat_axis=1, tiled=True)]
    all_to_all x1 -> x0, blocking collectives: 23.2 us -> none  [from_everyone(): lax.all_to_all(jnp.broadcast_to(value[None], (peers, *value.shape)), axis...]
    ppermute x3 -> x0, waiting for transfers between devices: 9.33 us -> none  [the longest x1 7.61 us: extended(): after = lax.ppermute(first, axis, down)]
    all_to_all x1 -> x0, starting transfers between devices: 8.13 us -> none  [on_device(): tile = lax.all_to_all(heat, 'src', split_axis=0, concat_axis=1, tiled=True)]
    reduce_sum x2 -> x0, other arithmetic: 7.78 us -> none  [the longest x1 7.69 us: on_device(): total = taken_together(jnp.sum(defect * defect, axis=(1, 2)), 'vtx')]
    ppermute x3 -> x0, starting transfers between devices: 6.72 us -> none  [the longest x1 4.02 us: extended(): before = lax.ppermute(last, axis, up)]
    all_to_all x1 -> x0, local copies, waits for them, and re-layouts: 4.62 us -> none  [on_device(): tile = lax.all_to_all(heat, 'src', split_axis=0, concat_axis=1, tiled=True)]
  transfers between devices with their start and end apart: 4 -> 0, of which waited for: 4 -> 0; matrix products, arithmetic and copies ran while one was open for 2% -> 0% of each run, Pallas kernels for 0% -> 0%
where the time goes in v1:
time: 81.7 us; the launch traced here: 81.4 us
  Pallas kernels  74.2 us (91%)
  local copies, waits for them, and re-layouts  4.07 us (5%)
  other arithmetic  2.48 us (3%)
    pallas_call x1, Pallas kernels, on_device(): pl.pallas_call(functools.partial(kernel, peers, amplitude), name='defect'...  74.2 us
    unnamed x8, local copies, waits for them, and re-layouts  4.07 us
    div x1, other arithmetic, on_device(): return (defect / norms[:, None, None], norms)  2.48 us

profile of v1, /device:TPU:1, one launch (start us, length us, event | category | flops | bytes accessed | tf_op | source)
XLA Modules:
  0.0 81.4 jit_solution(16624432172911545264)
XLA Ops:
  0.6 0.0 copy-start
  0.6 1.2 %copy-done = f32[4,8,8192]{2,1,0:T(8,128)S(1)} copy-done((f32[4,8,8192]{2,1,0:T(8,128)S(1)}, f32[4,8,8192]{2,1,0:T(8,128)}, u32[]{:S(2)}) %copy-start) | copy-done | bytes 1048600
  1.9 0.0 copy-start.1
  1.9 2.2 %copy-done.1 = f32[64,2,8192]{2,1,0:T(2,128)S(1)} copy-done((f32[64,2,8192]{2,1,0:T(2,128)S(1)}, f32[64,2,8192]{2,1,0:T(2,128)}, u32[]{:S(2)}) %copy-start.1) | copy-done | bytes 4194328
  4.0 0.0 copy-start.2
  4.0 0.7 copy-done.2
  4.7 74.2 %defect.1 = (f32[16,8,8192]{2,1,0:T(8,128)S(1)}, f32[1,128]{1,0:T(1,128)S(1)}) custom-call(f32[64,2,8192]{2,1,0:T(2,128)S(1)} %copy-done.1, f32[4,8,8192]{2,1,0:T(8,128)S(1)} %copy-done, f32[4,8,8192]{2,1,0:T(8,128)S(1)} %copy-done, s32[64]{0:T(128)S(1)} %copy-done.2), custom_call_target="tpu_custom_call" | custom-call | flops 200000000 | bytes 16000000 | tf_op jit(solution)/shard_map/defect/pallas_call | solution.py:493
  78.9 0.0 copy-start.3
  78.9 2.5 %broadcast_divide_fusion = f32[16,8,8192]{2,1,0:T(8,128)} fusion(f32[16,8,8192]{2,1,0:T(8,128)S(1)} %get-tuple-element.4, f32[16]{0:T(128)S(1)} %slice_bitcast_fusion), kind=kLoop, calls=%fused_computation | loop fusion | flops 1048576 | bytes 8388672 | tf_op jit(solution)/shard_map/div | solution.py:535
  81.4 0.0 copy-done.3
  (1 shorter events, 0.0 us)
Async XLA Ops:
  0.6 1.2 %copy-start = (f32[4,8,8192]{2,1,0:T(8,128)S(1)}, f32[4,8,8192]{2,1,0:T(8,128)}, u32[]{:S(2)}) copy-start(f32[4,8,8192]{2,1,0:T(8,128)} %cot.1) | copy-start | bytes 3145732
  1.9 2.2 %copy-start.1 = (f32[64,2,8192]{2,1,0:T(2,128)S(1)}, f32[64,2,8192]{2,1,0:T(2,128)}, u32[]{:S(2)}) copy-start(f32[64,2,8192]{2,1,0:T(2,128)} %heat.1) | copy-start | bytes 12582916
  4.0 0.7 copy-start.2
  78.9 2.5 %copy-start.3 = (f32[16]{0:T(128)}, f32[16]{0:T(128)S(1)}, u32[]{:S(2)}) copy-start(f32[16]{0:T(128)S(1)} %slice_bitcast_fusion) | copy-start | bytes 196

commit v2 on v0

v2 whole, which is shorter than its diff:
```python
import functools
import math

import jax
import jax.numpy as jnp
from jax import lax
from jax.experimental import pallas as pl
from jax.experimental.pallas import tpu as pltpu
from jax.sharding import PartitionSpec as P

MESH = pl.DeviceIdType.MESH
RING = 4
PLANE = 8
GROUP = 4
PIECE = 2
LATE = 1
LANES = 128
F32 = jnp.float32
ABOVE, BELOW = 8, 15


def at(v, k):
    return {"vtx": v, "src": k}


def remote(src, dst, send, recv, target):
    return pltpu.make_async_remote_copy(
        src_ref=src,
        dst_ref=dst,
        send_sem=send,
        recv_sem=recv,
        device_id=target,
        device_id_type=MESH,
    )


def signal(sem, target):
    pl.semaphore_signal(sem, inc=1, device_id=target, device_id_type=MESH)


def each(count, body):
    lax.fori_loop(0, count, lambda i, _: (body(i), 0)[1], 0)


def shifted_weights(cot, lower, weights, v, total_rows, width):
    tiles = width // LANES
    step = 8
    lane = lax.broadcasted_iota(jnp.int32, (8, LANES), 1)
    sub = lax.broadcasted_iota(jnp.int32, (8, LANES), 0)
    in_row = sub + 8 * v < total_rows - 1
    has_lower = jnp.full((8, LANES), v, jnp.int32) > 0
    zero = jnp.zeros((8, LANES), F32)

    def block(b, carry):
        for i in range(step):
            j = b * step + i
            cols = pl.ds(pl.multiple_of(j * LANES, LANES), LANES)
            in_col = lane + j * LANES < width - 1
            east = jnp.where(in_col, cot[1, :, cols], 0.0)
            north = jnp.where(in_row, cot[2, :, cols], 0.0)
            diag = jnp.where(in_col & in_row, cot[3, :, cols], 0.0)
            low_n = jnp.where(has_lower, lower[0, :, cols], 0.0)
            low_d = jnp.where(has_lower & in_col, lower[1, :, cols], 0.0)
            south = jnp.where(sub == 0, low_n, pltpu.roll(north, 1, 0))
            diag_s = jnp.where(sub == 0, low_d, pltpu.roll(diag, 1, 0))
            turned = tuple(pltpu.roll(w, 1, 1) for w in (east, diag, diag_s))
            west, diag_w, southwest = (
                jnp.where(lane == 0, left, here) for left, here in zip(carry, turned)
            )
            weights[0, :, cols] = (
                cot[0, :, cols] + east + west + north + south + diag + southwest
            )
            weights[1, :, cols] = north
            weights[2, :, cols] = south
            weights[3, :, cols] = east
            weights[4, :, cols] = west
            weights[5, :, cols] = diag_w
            weights[6, :, cols] = diag_s
            carry = turned
        return carry

    lax.fori_loop(0, tiles // step, block, (zero, zero, zero))


def field_defect(field, weights, out, s, where, amplitude, width):
    lane = lax.broadcasted_iota(jnp.int32, (8, LANES), 1)
    sub = lax.broadcasted_iota(jnp.int32, (8, LANES), 0)
    spot = where - (sub * width + lane)
    zero = jnp.zeros((8, LANES), F32)
    sums = [zero, zero]
    partial, east_at, west_at = None, None, zero

    def finish(j, to_left):
        done = partial - jnp.where(lane == LANES - 1, to_left, east_at)
        out[s, :, j * LANES : (j + 1) * LANES] = done
        sums[j % 2] = sums[j % 2] + done * done

    tiles = width // LANES
    for j in range(tiles):
        cols = slice(j * LANES, (j + 1) * LANES)
        h = field[s, 0:8, cols]
        halo = field[s, 8:16, cols]
        above = pltpu.roll(jnp.where(sub == 0, halo, h), 7, 0)
        below = pltpu.roll(jnp.where(sub == 7, halo, h), 1, 0)
        to_left = weights[4, :, cols] * h + weights[5, :, cols] * above
        to_right = weights[3, :, cols] * h + weights[6, :, cols] * below
        to_left = pltpu.roll(to_left, LANES - 1, 1)
        to_right = pltpu.roll(to_right, 1, 1)
        if j > 0:
            finish(j - 1, to_left)
        partial = (
            weights[0, :, cols] * h
            - weights[1, :, cols] * above
            - weights[2, :, cols] * below
            - jnp.where(lane == 0, west_at, to_right)
            - jnp.where(spot == j * LANES, amplitude, 0.0)
        )
        east_at, west_at = to_left, to_right
    finish(tiles - 1, zero)
    return sums[0] + sums[1]


def kernel(
    peers,
    amplitude,
    heat,
    cot_hbm,
    sources_hbm,
    out,
    norms,
    cot,
    sources,
    field,
    lower,
    weights,
    relay,
    row,
    rows,
    spare,
    known,
    own_sem,
    cot_sem,
    src_sem,
    low_send,
    low_recv,
    part_send,
    part_recv,
    hand_send,
    hand_recv,
    send,
    first_recv,
    near_recv,
    second_recv,
    edge_send,
    halo_send,
    halo_recv,
    relay_send,
    relay_recv,
    sum_send,
    sum_recv,
):
    v, k = lax.axis_index("vtx"), lax.axis_index("src")
    x = lax.rem(v, RING)
    per, _, width = field.shape
    groups, pieces = per // GROUP, per // PIECE
    up, down = lax.rem(v + 1, peers), lax.rem(v + peers - 1, peers)
    line = v - x
    top, bottom = k == 3, k == 0
    last, first = x == RING - 1, x == 0

    around = [line + lax.rem(x + i, RING) for i in range(1, RING)]
    across = v + RING - 2 * RING * lax.rem(v // RING, 2)
    depth = [lax.rem(v + PLANE, peers), lax.rem(v + peers - PLANE, peers)]
    shared = [at(v, k ^ q) for q in (2, 3, 1)]
    around, across, depth = (
        [at(i, k) for i in around],
        [at(across, k)],
        [at(i, k) for i in depth],
    )

    cot_copy = pltpu.make_async_copy(cot_hbm, cot, cot_sem)
    cot_copy.start()
    src_copy = pltpu.make_async_copy(sources_hbm, sources, src_sem)
    src_copy.start()
    own = pltpu.make_async_copy(
        heat.at[pl.ds(per * k, per)],
        field.at[:, pl.ds(pl.multiple_of(2 * k, 2), 2)],
        own_sem,
    )
    own.start()
    barrier = pltpu.get_barrier_semaphore()
    near = shared + around + across + depth
    for target in near:
        signal(barrier, target)
    pl.semaphore_wait(barrier, len(near))

    def some(start, count):
        return pl.ds(start, count)

    def arrived(ref, sem):
        pltpu.make_async_copy(ref, ref, sem).wait()

    edge_row = jnp.where(top, 1, 0)

    def exchange(i, q, r, start, count, sem):
        return remote(
            heat.at[pl.ds(per * (k ^ q) + start, count), r],
            field.at[some(start, count), 2 * k + r],
            send,
            sem,
            at(v, k ^ q),
        )

    def begin(g):
        for i, q in enumerate((2, 3)):
            exchange(i, q, edge_row, g * GROUP, GROUP, first_recv.at[g, i]).start()

    begin(0)

    above_side, below_side = last & (k >= 2), first & (k < 2)
    holds = top | bottom
    own_row = jnp.where(top, 1, 0)
    block_row = jnp.where(k >= 2, 7, 0)
    split = (above_side | below_side) & holds
    helps = (above_side | below_side) & jnp.logical_not(holds)
    handed = remote(
        heat.at[pl.ds(per * (k ^ 3), per), own_row],
        spare,
        hand_send,
        hand_recv,
        at(v, k ^ 1),
    )

    @pl.when(split)
    def _():
        handed.start()

    def begin_near(g):
        remote(
            heat.at[pl.ds(per * (k ^ 1) + g * GROUP, GROUP)],
            field.at[some(g * GROUP, GROUP), pl.ds(pl.multiple_of(2 * k, 2), 2)],
            send,
            near_recv.at[g],
            at(v, k ^ 1),
        ).start()

    each(groups, begin_near)

    def meet(stage, targets):
        for target in targets:
            signal(known.at[stage], target)
        pl.semaphore_wait(known.at[stage], len(targets))

    meet(0, around)
    meet(1, across)
    meet(2, shared)

    half = width // 2
    cut = pl.ds(pl.multiple_of(lax.rem(k, 2) * half, half), half)
    low = remote(
        cot_hbm.at[pl.ds(2, 2), 7, cut],
        lower.at[:, 0, cut],
        low_send,
        low_recv,
        at(up, k),
    )
    low.start()

    for g in range(groups):
        arrived(field.at[some(g * GROUP, GROUP), 0:2], near_recv.at[g])

    @pl.when(helps)
    def _():
        handed.wait_recv()

    def wrap_copies(c):
        via = lax.rem(c, RING)
        slot = c // RING
        span = some(c * PIECE, PIECE)
        sem = c * PIECE // GROUP

        def send_on(src, m):
            for side, active, end, hop in (
                (0, above_side, 0, up),
                (1, below_side, RING - 1, down - (RING - 1)),
            ):

                @pl.when(active & (via == end))
                def _():
                    remote(
                        src,
                        field.at[span, (BELOW, ABOVE)[side]],
                        edge_send,
                        halo_recv.at[sem, side],
                        at(hop + via, m),
                    ).start()

                @pl.when(active & (via != end))
                def _():
                    remote(
                        src,
                        relay.at[side, slot],
                        edge_send,
                        relay_recv.at[side, slot],
                        at(hop + via, m),
                    ).start()

        @pl.when(split)
        def _():
            for m in (k, k ^ 2):
                send_on(heat.at[pl.ds(per * m + c * PIECE, PIECE), own_row], m)

        @pl.when(helps)
        def _():
            send_on(field.at[span, block_row], k)
            send_on(spare.at[span], k ^ 2)

    each(pieces, wrap_copies)

    def edge_copies(g):
        span = some(g * GROUP, GROUP)
        for i in range(2):

            @pl.when(top & jnp.logical_not(last))
            def _():
                m = 2 + i
                remote(
                    heat.at[pl.ds(per * m + g * GROUP, GROUP), 1],
                    field.at[span, BELOW],
                    edge_send,
                    halo_recv.at[g, 0],
                    at(up, m),
                ).start()

            @pl.when(bottom & jnp.logical_not(first))
            def _():
                remote(
                    heat.at[pl.ds(per * i + g * GROUP, GROUP), 0],
                    field.at[span, ABOVE],
                    edge_send,
                    halo_recv.at[g, 1],
                    at(down, i),
                ).start()

    each(groups, edge_copies)

    lax.fori_loop(1, groups, lambda g, _: (begin(g), 0)[1], 0)

    def begin_second(b):
        for i, q in enumerate((2, 3)):
            exchange(
                i, q, 1 - edge_row, b * LATE, LATE, second_recv.at[b, i]
            ).start()

    each(per // LATE, begin_second)

    arrived(lower.at[:, 0, cut], low_recv)
    part = remote(
        lower.at[:, 0, cut], lower.at[:, 0, cut], part_send, part_recv, at(v, k ^ 1)
    )
    part.start()
    cot_copy.wait()
    src_copy.wait()
    part.wait_recv()
    shifted_weights(cot, lower, weights, v, peers * 8, width)
    meet(3, depth)

    came = jnp.where((k == 0) | (k == 3), 1, 0)
    inner_up = (k < 2) & jnp.logical_not(last)
    inner_down = (k >= 2) & jnp.logical_not(first)

    def forward(g):
        span = some(g * GROUP, GROUP)

        @pl.when(inner_up)
        def _():
            remote(
                field.at[span, 7],
                field.at[span, BELOW],
                halo_send,
                halo_recv.at[g, 0],
                at(up, k),
            ).start()

        @pl.when(inner_down)
        def _():
            remote(
                field.at[span, 0],
                field.at[span, ABOVE],
                halo_send,
                halo_recv.at[g, 1],
                at(down, k),
            ).start()

    def relayed(slot):
        c = x + RING * slot
        span = some(c * PIECE, PIECE)
        sem = c * PIECE // GROUP

        @pl.when(jnp.logical_not(first))
        def _():
            arrived(relay.at[0, slot], relay_recv.at[0, slot])
            remote(
                relay.at[0, slot],
                field.at[span, BELOW],
                relay_send.at[0],
                halo_recv.at[sem, 0],
                at(line, k),
            ).start()

        @pl.when(jnp.logical_not(last))
        def _():
            arrived(relay.at[1, slot], relay_recv.at[1, slot])
            remote(
                relay.at[1, slot],
                field.at[span, ABOVE],
                relay_send.at[1],
                halo_recv.at[sem, 1],
                at(line + RING - 1, k),
            ).start()

    for g in range(groups):
        arrived(field.at[some(g * GROUP, GROUP), 0], first_recv.at[g, came])
        forward(g)
        if g % 2 == 1:
            meet(4 + g // 2, depth)

    own.wait()
    lane = lax.broadcasted_iota(jnp.int32, (1, LANES), 1)
    base = v * (8 * width)

    slots = pieces // RING

    def group(g, sums):
        span = some(g * GROUP, GROUP)

        @pl.when(lax.rem(g, groups // slots) == 0)
        def _():
            relayed(g // (groups // slots))

        arrived(field.at[span, 0], first_recv.at[g, 1 - came])
        for i in range(2):
            arrived(field.at[span, 0], halo_recv.at[g, i])

        def late(b, sums):
            for i in range(2):
                arrived(field.at[some(b * LATE, LATE), 0], second_recv.at[b, i])

            def one(s, sums):
                acc = field_defect(
                    field,
                    weights,
                    out,
                    s,
                    sources[per * k + s] - base,
                    amplitude,
                    width,
                )
                total = jnp.sum(acc, axis=(0, 1), keepdims=True)
                return sums + jnp.where(lane == s, total, 0.0)

            return lax.fori_loop(b * LATE, (b + 1) * LATE, one, sums)

        share = GROUP // LATE
        return lax.fori_loop(g * share, (g + 1) * share, late, sums)

    sums = lax.fori_loop(0, groups, group, jnp.zeros((1, LANES), F32))

    row[...] = sums

    def tell(i):
        remote(row, rows.at[i], sum_send, sum_recv, at(lax.rem(v + i, peers), k)).start()

    lax.fori_loop(1, peers, lambda i, _: (tell(i), 0)[1], 0)

    low.wait_send()
    part.wait_send()
    sizes = (field.at[0 : 3 * per // 4, 0:8], send)
    arrived(*sizes)

    @pl.when(split)
    def _():
        handed.wait_send()

    wraps = above_side | below_side
    inner = (top & jnp.logical_not(last)) | (bottom & jnp.logical_not(first))

    @pl.when(wraps | inner)
    def _():
        arrived(field.at[:, 0:2], edge_send)

    @pl.when(inner_up | inner_down)
    def _():
        arrived(field.at[:, 0:1], halo_send)

    @pl.when(jnp.logical_not(first))
    def _():
        arrived(relay.at[0], relay_send.at[0])

    @pl.when(jnp.logical_not(last))
    def _():
        arrived(relay.at[1], relay_send.at[1])

    arrived(rows.at[1:peers], sum_recv)
    sums = sums + jnp.sum(rows[1:peers], axis=0)
    norms[...] = jnp.sqrt(sums / (peers * 8 * width) + 1e-06)
    arrived(rows.at[1:peers], sum_send)


def scale(defect, norms, out, held, sem):
    per = defect.shape[0]
    lane = lax.broadcasted_iota(jnp.int32, (per, LANES), 1)
    which = lax.broadcasted_iota(jnp.int32, (per, LANES), 0)
    own = jnp.where(lane == which, norms[...], 0.0)
    inverse = 1.0 / jnp.sum(own, axis=1, keepdims=True)
    copies = []
    for s in range(per):
        held[s] = defect[s] * inverse[s : s + 1]
        copies.append(pltpu.make_async_copy(held.at[s], out.at[s], sem.at[s]))
        copies[-1].start()
    for copy in copies:
        copy.wait()


def on_device(heat, cotan, source_index):
    peers = lax.axis_size("vtx")
    rows_dev, width = cotan.shape[1:]
    per = heat.shape[0] // lax.axis_size("src")
    groups, slots = per // GROUP, per // PIECE // RING
    amplitude = math.sqrt(rows_dev * peers * width) / 8.0
    dma, vmem = pltpu.SemaphoreType.DMA, pltpu.VMEM
    anywhere = pl.BlockSpec(memory_space=pl.ANY)
    held = pl.BlockSpec(memory_space=pltpu.VMEM)
    block = jax.ShapeDtypeStruct((per, rows_dev, width), F32)
    defect, norms = pl.pallas_call(
        functools.partial(kernel, peers, amplitude),
        name="defect",
        out_shape=(block, jax.ShapeDtypeStruct((1, LANES), F32)),
        in_specs=[anywhere] * 3,
        out_specs=(held, held),
        scratch_shapes=[
            vmem((4, rows_dev, width), F32),
            pltpu.SMEM(source_index.shape, jnp.int32),
            vmem((per, 2 * rows_dev, width), F32),
            vmem((2, 8, width), F32),
            vmem((7, rows_dev, width), F32),
            vmem((2, slots, PIECE, width), F32),
            vmem((1, LANES), F32),
            vmem((peers, 1, LANES), F32),
            vmem((per, width), F32),
            pltpu.SemaphoreType.REGULAR((6,)),
            dma,
            dma,
            dma,
            dma,
            dma,
            dma,
            dma,
            dma,
            dma,
            dma,
            dma((groups, 2)),
            dma((groups,)),
            dma((per // LATE, 2)),
            dma,
            dma,
            dma((groups, 2)),
            dma((2,)),
            dma((2, slots)),
            dma,
            dma,
        ],
        compiler_params=pltpu.CompilerParams(
            collective_id=0, has_side_effects=True, vmem_limit_bytes=40 << 20
        ),
        cost_estimate=pl.CostEstimate(
            flops=200_000_000, bytes_accessed=16_000_000, transcendentals=0
        ),
    )(
        *(
            pltpu.with_memory_space_constraint(a, pltpu.HBM)
            for a in (heat, cotan, source_index)
        )
    )
    norms, col_norm = lax.optimization_barrier((norms, norms[0, :per]))
    normalised = pl.pallas_call(
        scale,
        name="scale",
        out_shape=block,
        in_specs=[held, held],
        out_specs=anywhere,
        scratch_shapes=[vmem(block.shape, F32), dma((per,))],
        compiler_params=pltpu.CompilerParams(vmem_limit_bytes=16 << 20),
    )(defect, norms)
    return (normalised, col_norm)


def solution(mesh):
    return jax.shard_map(
        on_device,
        mesh=mesh,
        in_specs=(P(None, ("vtx", "src"), None), P(None, "vtx", None), P()),
        out_specs=(P("src", "vtx", None), P("src")),
        check_vma=False,
    )
```

time: 119 us -> 72.2 us (0.61); the launches traced: 117 us -> 72.2 us
  Pallas kernels: 0 us -> 71 us
  waiting for transfers between devices: 56.3 us -> 0 us
  blocking collectives: 23.2 us -> 0 us
  starting transfers between devices: 14.9 us -> 0 us
  other arithmetic: 11.2 us -> 0 us
  local copies, waits for them, and re-layouts: 10.9 us -> 0.51 us
    pallas_call x0 -> x2, Pallas kernels: none -> 71 us  [the longest x1 68.8 us: on_device(): pl.pallas_call(functools.partial(kernel, peers, amplitude), name='defect'...]
    all_to_all x1 -> x0, waiting for transfers between devices: 46.9 us -> none  [on_device(): tile = lax.all_to_all(heat, 'src', split_axis=0, concat_axis=1, tiled=True)]
    all_to_all x1 -> x0, blocking collectives: 23.2 us -> none  [from_everyone(): lax.all_to_all(jnp.broadcast_to(value[None], (peers, *value.shape)), axis...]
    ppermute x3 -> x0, waiting for transfers between devices: 9.33 us -> none  [the longest x1 7.61 us: extended(): after = lax.ppermute(first, axis, down)]
    all_to_all x1 -> x0, starting transfers between devices: 8.13 us -> none  [on_device(): tile = lax.all_to_all(heat, 'src', split_axis=0, concat_axis=1, tiled=True)]
    reduce_sum x2 -> x0, other arithmetic: 7.78 us -> none  [the longest x1 7.69 us: on_device(): total = taken_together(jnp.sum(defect * defect, axis=(1, 2)), 'vtx')]
    ppermute x3 -> x0, starting transfers between devices: 6.72 us -> none  [the longest x1 4.02 us: extended(): before = lax.ppermute(last, axis, up)]
    all_to_all x1 -> x0, local copies, waits for them, and re-layouts: 4.62 us -> none  [on_device(): tile = lax.all_to_all(heat, 'src', split_axis=0, concat_axis=1, tiled=True)]
  transfers between devices with their start and end apart: 4 -> 0, of which waited for: 4 -> 0; matrix products, arithmetic and copies ran while one was open for 2% -> 0% of each run, Pallas kernels for 0% -> 0%
where the time goes in v2:
time: 72.2 us
  Pallas kernels  71 us (98%)
    pallas_call x1, Pallas kernels, on_device(): pl.pallas_call(functools.partial(kernel, peers, amplitude), name='defect'...  68.8 us
    pallas_call x1, Pallas kernels, on_device(): pl.pallas_call(scale, name='scale', out_shape=block, in_specs=[held, held...  2.23 us

profile of v2, /device:TPU:1, one launch (start us, length us, event | category | flops | bytes accessed | tf_op | source)
XLA Modules:
  0.0 72.2 jit_solution(1473899889637385553)
XLA Ops:
  0.6 68.8 %defect.1 = (f32[16,8,8192]{2,1,0:T(8,128)S(1)}, f32[1,128]{1,0:T(1,128)S(1)}) custom-call(f32[64,2,8192]{2,1,0:T(2,128)} %heat.1, f32[4,8,8192]{2,1,0:T(8,128)} %cot_hbm.1, s32[64]{0:T(128)} %sources_hbm.1), custom_call_target="tpu_custom_call" | custom-call | flops 200000000 | bytes 16000000 | tf_op jit(solution)/shard_map/defect/pallas_call | solution.py:535
  69.4 0.5 slice_bitcast_fusion
  69.9 2.2 %scale.1 = f32[16,8,8192]{2,1,0:T(8,128)} custom-call(f32[16,8,8192]{2,1,0:T(8,128)S(1)} %get-tuple-element.6.defect, f32[1,128]{1,0:T(1,128)S(1)} %get-tuple-element.8.norms), custom_call_target="tpu_custom_call" | custom-call | tf_op jit(solution)/shard_map/scale/pallas_call | solution.py:586

commit v3 on v2

--- a/solution.py
+++ b/solution.py
@@ -13,7 +13,7 @@
 PLANE = 8
 GROUP = 4
 PIECE = 2
-LATE = 1
+TELL = 9
 LANES = 128
 F32 = jnp.float32
 ABOVE, BELOW = 8, 15
@@ -143,9 +143,7 @@
     src_sem,
     low_send,
     low_recv,
-    part_send,
     part_recv,
-    hand_send,
     hand_recv,
     send,
     first_recv,
@@ -163,6 +161,7 @@
     x = lax.rem(v, RING)
     per, _, width = field.shape
     groups, pieces = per // GROUP, per // PIECE
+    tail = per - GROUP
     up, down = lax.rem(v + 1, peers), lax.rem(v + peers - 1, peers)
     line = v - x
     top, bottom = k == 3, k == 0
@@ -202,7 +201,7 @@
 
     edge_row = jnp.where(top, 1, 0)
 
-    def exchange(i, q, r, start, count, sem):
+    def exchange(q, r, start, count, sem):
         return remote(
             heat.at[pl.ds(per * (k ^ q) + start, count), r],
             field.at[some(start, count), 2 * k + r],
@@ -212,12 +211,13 @@
         )
 
     def begin(g):
-        for i, q in enumerate((2, 3)):
-            exchange(i, q, edge_row, g * GROUP, GROUP, first_recv.at[g, i]).start()
+        for q in (2, 3):
+            exchange(q, edge_row, g * GROUP, GROUP, first_recv.at[g]).start()
 
     begin(0)
 
-    above_side, below_side = last & (k >= 2), first & (k < 2)
+    above_side = last & (k >= 2)
+    below_side = first & (k < 2)
     holds = top | bottom
     own_row = jnp.where(top, 1, 0)
     block_row = jnp.where(k >= 2, 7, 0)
@@ -226,7 +226,7 @@
     handed = remote(
         heat.at[pl.ds(per * (k ^ 3), per), own_row],
         spare,
-        hand_send,
+        edge_send,
         hand_recv,
         at(v, k ^ 1),
     )
@@ -240,7 +240,7 @@
             heat.at[pl.ds(per * (k ^ 1) + g * GROUP, GROUP)],
             field.at[some(g * GROUP, GROUP), pl.ds(pl.multiple_of(2 * k, 2), 2)],
             send,
-            near_recv.at[g],
+            near_recv,
             at(v, k ^ 1),
         ).start()
 
@@ -266,8 +266,7 @@
     )
     low.start()
 
-    for g in range(groups):
-        arrived(field.at[some(g * GROUP, GROUP), 0:2], near_recv.at[g])
+    arrived(field.at[:, 0:2], near_recv)
 
     @pl.when(helps)
     def _():
@@ -291,7 +290,7 @@
                         src,
                         field.at[span, (BELOW, ABOVE)[side]],
                         edge_send,
-                        halo_recv.at[sem, side],
+                        halo_recv.at[sem],
                         at(hop + via, m),
                     ).start()
 
@@ -328,7 +327,7 @@
                     heat.at[pl.ds(per * m + g * GROUP, GROUP), 1],
                     field.at[span, BELOW],
                     edge_send,
-                    halo_recv.at[g, 0],
+                    halo_recv.at[g],
                     at(up, m),
                 ).start()
 
@@ -338,7 +337,7 @@
                     heat.at[pl.ds(per * i + g * GROUP, GROUP), 0],
                     field.at[span, ABOVE],
                     edge_send,
-                    halo_recv.at[g, 1],
+                    halo_recv.at[g],
                     at(down, i),
                 ).start()
 
@@ -346,17 +345,21 @@
 
     lax.fori_loop(1, groups, lambda g, _: (begin(g), 0)[1], 0)
 
-    def begin_second(b):
-        for i, q in enumerate((2, 3)):
-            exchange(
-                i, q, 1 - edge_row, b * LATE, LATE, second_recv.at[b, i]
-            ).start()
-
-    each(per // LATE, begin_second)
+    def begin_second(g):
+        for q in (2, 3):
+            exchange(q, 1 - edge_row, g * GROUP, GROUP, second_recv.at[g]).start()
+
+    each(groups - 1, begin_second)
+
+    def begin_last(n):
+        for q in (2, 3):
+            exchange(q, 1 - edge_row, tail + n, 1, second_recv.at[groups - 1 + n]).start()
+
+    each(GROUP, begin_last)
 
     arrived(lower.at[:, 0, cut], low_recv)
     part = remote(
-        lower.at[:, 0, cut], lower.at[:, 0, cut], part_send, part_recv, at(v, k ^ 1)
+        lower.at[:, 0, cut], lower.at[:, 0, cut], low_send, part_recv, at(v, k ^ 1)
     )
     part.start()
     cot_copy.wait()
@@ -365,7 +368,6 @@
     shifted_weights(cot, lower, weights, v, peers * 8, width)
     meet(3, depth)
 
-    came = jnp.where((k == 0) | (k == 3), 1, 0)
     inner_up = (k < 2) & jnp.logical_not(last)
     inner_down = (k >= 2) & jnp.logical_not(first)
 
@@ -378,7 +380,7 @@
                 field.at[span, 7],
                 field.at[span, BELOW],
                 halo_send,
-                halo_recv.at[g, 0],
+                halo_recv.at[g],
                 at(up, k),
             ).start()
 
@@ -388,39 +390,44 @@
                 field.at[span, 0],
                 field.at[span, ABOVE],
                 halo_send,
-                halo_recv.at[g, 1],
+                halo_recv.at[g],
                 at(down, k),
             ).start()
+
+    relays_up = jnp.logical_not(first)
+    relays_down = jnp.logical_not(last)
 
     def relayed(slot):
         c = x + RING * slot
         span = some(c * PIECE, PIECE)
         sem = c * PIECE // GROUP
 
-        @pl.when(jnp.logical_not(first))
+        @pl.when(relays_up)
         def _():
             arrived(relay.at[0, slot], relay_recv.at[0, slot])
             remote(
                 relay.at[0, slot],
                 field.at[span, BELOW],
                 relay_send.at[0],
-                halo_recv.at[sem, 0],
+                halo_recv.at[sem],
                 at(line, k),
             ).start()
 
-        @pl.when(jnp.logical_not(last))
+        @pl.when(relays_down)
         def _():
             arrived(relay.at[1, slot], relay_recv.at[1, slot])
             remote(
                 relay.at[1, slot],
                 field.at[span, ABOVE],
                 relay_send.at[1],
-                halo_recv.at[sem, 1],
+                halo_recv.at[sem],
                 at(line + RING - 1, k),
             ).start()
 
     for g in range(groups):
-        arrived(field.at[some(g * GROUP, GROUP), 0], first_recv.at[g, came])
+        if g == groups - 1:
+            relayed(0)
+        arrived(field.at[some(g * GROUP, GROUP), 0:2], first_recv.at[g])
         forward(g)
         if g % 2 == 1:
             meet(4 + g // 2, depth)
@@ -429,63 +436,64 @@
     lane = lax.broadcasted_iota(jnp.int32, (1, LANES), 1)
     base = v * (8 * width)
 
-    slots = pieces // RING
-
     def group(g, sums):
         span = some(g * GROUP, GROUP)
 
-        @pl.when(lax.rem(g, groups // slots) == 0)
-        def _():
-            relayed(g // (groups // slots))
-
-        arrived(field.at[span, 0], first_recv.at[g, 1 - came])
-        for i in range(2):
-            arrived(field.at[span, 0], halo_recv.at[g, i])
-
-        def late(b, sums):
-            for i in range(2):
-                arrived(field.at[some(b * LATE, LATE), 0], second_recv.at[b, i])
-
-            def one(s, sums):
-                acc = field_defect(
-                    field,
-                    weights,
-                    out,
-                    s,
-                    sources[per * k + s] - base,
-                    amplitude,
-                    width,
-                )
-                total = jnp.sum(acc, axis=(0, 1), keepdims=True)
-                return sums + jnp.where(lane == s, total, 0.0)
-
-            return lax.fori_loop(b * LATE, (b + 1) * LATE, one, sums)
-
-        share = GROUP // LATE
-        return lax.fori_loop(g * share, (g + 1) * share, late, sums)
+        @pl.when(g == 1)
+        def _():
+            relayed(1)
+
+        arrived(field.at[span, 0:2], halo_recv.at[g])
+        only = g < groups - 1
+
+        @pl.when(only)
+        def _():
+            arrived(field.at[span, 0:2], second_recv.at[g])
+
+        def one(s, sums):
+            @pl.when(jnp.logical_not(only))
+            def _():
+                arrived(field.at[pl.ds(s, 1), 0:2], second_recv.at[groups - 1 + s - tail])
+
+            acc = field_defect(
+                field,
+                weights,
+                out,
+                s,
+                sources[per * k + s] - base,
+                amplitude,
+                width,
+            )
+            total = jnp.sum(acc, axis=(0, 1), keepdims=True)
+            return sums + jnp.where(lane == s, total, 0.0)
+
+        return lax.fori_loop(g * GROUP, (g + 1) * GROUP, one, sums)
 
     sums = lax.fori_loop(0, groups, group, jnp.zeros((1, LANES), F32))
 
     row[...] = sums
 
-    def tell(i):
-        remote(row, rows.at[i], sum_send, sum_recv, at(lax.rem(v + i, peers), k)).start()
-
-    lax.fori_loop(1, peers, lambda i, _: (tell(i), 0)[1], 0)
-
-    low.wait_send()
-    part.wait_send()
-    sizes = (field.at[0 : 3 * per // 4, 0:8], send)
-    arrived(*sizes)
+    def tell(n, _):
+        i = 1 + lax.rem(peers // 2 + TELL * n, peers - 1)
+        for step in range(TELL):
+            i_step = lax.rem(i + step - 1, peers - 1) + 1
+            remote(
+                row, rows.at[i_step], sum_send, sum_recv, at(lax.rem(v + i_step, peers), k)
+            ).start()
+        return 0
+
+    lax.fori_loop(0, (peers - 1) // TELL, tell, 0)
+
+    arrived(lower.at[:, 0], low_send)
+    arrived(field.at[0 : 3 * per // 4, 0:8], send)
+
+    inner = (top & jnp.logical_not(last)) | (bottom & jnp.logical_not(first))
 
     @pl.when(split)
     def _():
-        handed.wait_send()
-
-    wraps = above_side | below_side
-    inner = (top & jnp.logical_not(last)) | (bottom & jnp.logical_not(first))
-
-    @pl.when(wraps | inner)
+        arrived(field.at[:, 0:3], edge_send)
+
+    @pl.when(helps | inner)
     def _():
         arrived(field.at[:, 0:2], edge_send)
 
@@ -493,11 +501,11 @@
     def _():
         arrived(field.at[:, 0:1], halo_send)
 
-    @pl.when(jnp.logical_not(first))
+    @pl.when(relays_up)
     def _():
         arrived(relay.at[0], relay_send.at[0])
 
-    @pl.when(jnp.logical_not(last))
+    @pl.when(relays_down)
     def _():
         arrived(relay.at[1], relay_send.at[1])
 
@@ -509,9 +517,9 @@
 
 def scale(defect, norms, out, held, sem):
     per = defect.shape[0]
-    lane = lax.broadcasted_iota(jnp.int32, (per, LANES), 1)
-    which = lax.broadcasted_iota(jnp.int32, (per, LANES), 0)
-    own = jnp.where(lane == which, norms[...], 0.0)
+    lane = lax.broadcasted_iota(jnp.int32, (per, per), 1)
+    which = lax.broadcasted_iota(jnp.int32, (per, per), 0)
+    own = jnp.where(lane == which, norms[...][None, :], 0.0)
     inverse = 1.0 / jnp.sum(own, axis=1, keepdims=True)
     copies = []
     for s in range(per):
@@ -549,22 +557,13 @@
             vmem((peers, 1, LANES), F32),
             vmem((per, width), F32),
             pltpu.SemaphoreType.REGULAR((6,)),
+            *[dma] * 8,
+            dma((groups,)),
+            dma,
+            dma((groups - 1 + GROUP,)),
             dma,
             dma,
-            dma,
-            dma,
-            dma,
-            dma,
-            dma,
-            dma,
-            dma,
-            dma,
-            dma((groups, 2)),
             dma((groups,)),
-            dma((per // LATE, 2)),
-            dma,
-            dma,
-            dma((groups, 2)),
             dma((2,)),
             dma((2, slots)),
             dma,
@@ -582,7 +581,7 @@
             for a in (heat, cotan, source_index)
         )
     )
-    norms, col_norm = lax.optimization_barrier((norms, norms[0, :per]))
+    norms = norms[0, :per]
     normalised = pl.pallas_call(
         scale,
         name="scale",
@@ -591,8 +590,11 @@
         out_specs=anywhere,
         scratch_shapes=[vmem(block.shape, F32), dma((per,))],
         compiler_params=pltpu.CompilerParams(vmem_limit_bytes=16 << 20),
+        cost_estimate=pl.CostEstimate(
+            flops=4_000_000, bytes_accessed=8_400_000, transcendentals=0
+        ),
     )(defect, norms)
-    return (normalised, col_norm)
+    return (normalised, norms)
 
 
 def solution(mesh):

time: 72.2 us -> 71.7 us (level)
  no operation moved by 1% of the time
where the time goes in v3:
time: 71.7 us; the launch traced here: 71.6 us
  Pallas kernels  70.9 us (99%)
    pallas_call x1, Pallas kernels, on_device(): pl.pallas_call(functools.partial(kernel, peers, amplitude), name='defect'...  68.6 us
    pallas_call x1, Pallas kernels, on_device(): pl.pallas_call(scale, name='scale', out_shape=block, in_specs=[held, held...  2.29 us

profile of v3, /device:TPU:1, one launch (start us, length us, event | category | flops | bytes accessed | tf_op | source)
XLA Modules:
  0.0 71.6 jit_solution(6058825195099755577)
XLA Ops:
  0.6 68.6 %defect.1 = (f32[16,8,8192]{2,1,0:T(8,128)S(1)}, f32[1,128]{1,0:T(1,128)S(1)}) custom-call(f32[64,2,8192]{2,1,0:T(2,128)} %heat.1, f32[4,8,8192]{2,1,0:T(8,128)} %cot_hbm.1, s32[64]{0:T(128)} %sources_hbm.1), custom_call_target="tpu_custom_call" | custom-call | flops 200000000 | bytes 16000000 | tf_op jit(solution)/shard_map/defect/pallas_call | solution.py:543
  69.3 0.0 copy-start
  69.3 2.3 %scale.1 = f32[16,8,8192]{2,1,0:T(8,128)} custom-call(f32[16,8,8192]{2,1,0:T(8,128)S(1)} %get-tuple-element.4.defect, f32[16]{0:T(128)S(1)} %slice_bitcast_fusion.norms), custom_call_target="tpu_custom_call" | custom-call | flops 4000000 | bytes 8400000 | tf_op jit(solution)/shard_map/scale/pallas_call | solution.py:585
  71.6 0.0 copy-done
  (1 shorter events, 0.0 us)
Async XLA Ops:
  69.3 2.3 %copy-start = (f32[16]{0:T(128)}, f32[16]{0:T(128)S(1)}, u32[]{:S(2)}) copy-start(f32[16]{0:T(128)S(1)} %slice_bitcast_fusion.norms) | copy-start | bytes 196

commit v4 on v3

--- a/solution.py
+++ b/solution.py
@@ -137,7 +137,9 @@
     row,
     rows,
     spare,
+    stage,
     known,
+    stage_sem,
     own_sem,
     cot_sem,
     src_sem,
@@ -177,6 +179,20 @@
         [at(i, k) for i in depth],
     )
 
+    barrier = pltpu.get_barrier_semaphore()
+    near = shared + around + across + depth
+    for target in near:
+        signal(barrier, target)
+    other = [2 - 2 * (k // 2) + core for core in range(2)]
+    edge_row = jnp.where(top, 1, 0)
+    staged = [
+        pltpu.make_async_copy(
+            heat.at[pl.ds(per * to, GROUP), edge_row], stage.at[i], stage_sem.at[i]
+        )
+        for i, to in enumerate(other)
+    ]
+    for copy in staged:
+        copy.start()
     cot_copy = pltpu.make_async_copy(cot_hbm, cot, cot_sem)
     cot_copy.start()
     src_copy = pltpu.make_async_copy(sources_hbm, sources, src_sem)
@@ -187,10 +203,6 @@
         own_sem,
     )
     own.start()
-    barrier = pltpu.get_barrier_semaphore()
-    near = shared + around + across + depth
-    for target in near:
-        signal(barrier, target)
     pl.semaphore_wait(barrier, len(near))
 
     def some(start, count):
@@ -199,22 +211,28 @@
     def arrived(ref, sem):
         pltpu.make_async_copy(ref, ref, sem).wait()
 
-    edge_row = jnp.where(top, 1, 0)
-
-    def exchange(q, r, start, count, sem):
+    def exchange(to, r, start, count, sem):
         return remote(
-            heat.at[pl.ds(per * (k ^ q) + start, count), r],
+            heat.at[pl.ds(per * to + start, count), r],
             field.at[some(start, count), 2 * k + r],
             send,
             sem,
-            at(v, k ^ q),
+            at(v, to),
         )
 
     def begin(g):
-        for q in (2, 3):
-            exchange(q, edge_row, g * GROUP, GROUP, first_recv.at[g]).start()
-
-    begin(0)
+        for to in other:
+            exchange(to, edge_row, g * GROUP, GROUP, first_recv.at[g]).start()
+
+    for i, to in enumerate(other):
+        staged[i].wait()
+        remote(
+            stage.at[i],
+            field.at[0:GROUP, 2 * k + edge_row],
+            send,
+            first_recv.at[0],
+            at(v, to),
+        ).start()
 
     above_side = last & (k >= 2)
     below_side = first & (k < 2)
@@ -346,16 +364,17 @@
     lax.fori_loop(1, groups, lambda g, _: (begin(g), 0)[1], 0)
 
     def begin_second(g):
-        for q in (2, 3):
-            exchange(q, 1 - edge_row, g * GROUP, GROUP, second_recv.at[g]).start()
+        for to in other:
+            exchange(to, 1 - edge_row, g * GROUP, GROUP, second_recv.at[g]).start()
 
     each(groups - 1, begin_second)
 
-    def begin_last(n):
-        for q in (2, 3):
-            exchange(q, 1 - edge_row, tail + n, 1, second_recv.at[groups - 1 + n]).start()
-
-    each(GROUP, begin_last)
+    def begin_last(n, to):
+        exchange(to, 1 - edge_row, tail + n, 1, second_recv.at[groups - 1 + n]).start()
+
+    for to in other:
+        for n in range(GROUP):
+            begin_last(n, to)
 
     arrived(lower.at[:, 0, cut], low_recv)
     part = remote(
@@ -474,9 +493,9 @@
     row[...] = sums
 
     def tell(n, _):
-        i = 1 + lax.rem(peers // 2 + TELL * n, peers - 1)
+        far = peers // 2 + PLANE - 1
         for step in range(TELL):
-            i_step = lax.rem(i + step - 1, peers - 1) + 1
+            i_step = 1 + lax.rem(far + peers - 2 - TELL * n - step, peers - 1)
             remote(
                 row, rows.at[i_step], sum_send, sum_recv, at(lax.rem(v + i_step, peers), k)
             ).start()
@@ -556,7 +575,9 @@
             vmem((1, LANES), F32),
             vmem((peers, 1, LANES), F32),
             vmem((per, width), F32),
+            vmem((2, GROUP, width), F32),
             pltpu.SemaphoreType.REGULAR((6,)),
+            dma((2,)),
             *[dma] * 8,
             dma((groups,)),
             dma,

time: 71.7 us -> 71 us (level)
  no operation moved by 1% of the time
where the time goes in v4:
time: 71 us; the launch traced here: 70.9 us
  Pallas kernels  70.3 us (99%)
    pallas_call x1, Pallas kernels, on_device(): pl.pallas_call(functools.partial(kernel, peers, amplitude), name='defect'...  68 us
    pallas_call x1, Pallas kernels, on_device(): pl.pallas_call(scale, name='scale', out_shape=block, in_specs=[held, held...  2.29 us

profile of v4, /device:TPU:1, one launch (start us, length us, event | category | flops | bytes accessed | tf_op | source)
XLA Modules:
  0.0 70.9 jit_solution(16897214356498212667)
XLA Ops:
  0.6 68.0 %defect.1 = (f32[16,8,8192]{2,1,0:T(8,128)S(1)}, f32[1,128]{1,0:T(1,128)S(1)}) custom-call(f32[64,2,8192]{2,1,0:T(2,128)} %heat.1, f32[4,8,8192]{2,1,0:T(8,128)} %cot_hbm.1, s32[64]{0:T(128)} %sources_hbm.1), custom_call_target="tpu_custom_call" | custom-call | flops 200000000 | bytes 16000000 | tf_op jit(solution)/shard_map/defect/pallas_call | solution.py:562
  68.6 0.0 copy-start
  68.6 2.3 %scale.1 = f32[16,8,8192]{2,1,0:T(8,128)} custom-call(f32[16,8,8192]{2,1,0:T(8,128)S(1)} %get-tuple-element.4.defect, f32[16]{0:T(128)S(1)} %slice_bitcast_fusion.norms), custom_call_target="tpu_custom_call" | custom-call | flops 4000000 | bytes 8400000 | tf_op jit(solution)/shard_map/scale/pallas_call | solution.py:606
  70.9 0.0 copy-done
  (1 shorter events, 0.0 us)
Async XLA Ops:
  68.6 2.3 %copy-start = (f32[16]{0:T(128)}, f32[16]{0:T(128)S(1)}, u32[]{:S(2)}) copy-start(f32[16]{0:T(128)S(1)} %slice_bitcast_fusion.norms) | copy-start | bytes 196

commit v5 on v4

--- a/solution.py
+++ b/solution.py
@@ -13,6 +13,7 @@
 PLANE = 8
 GROUP = 4
 PIECE = 2
+STOPS = (0, 1, 3, 6, 9, 12, 15)
 TELL = 9
 LANES = 128
 F32 = jnp.float32
@@ -183,7 +184,7 @@
     near = shared + around + across + depth
     for target in near:
         signal(barrier, target)
-    other = [2 - 2 * (k // 2) + core for core in range(2)]
+    other = [2 - 2 * (k // 2) + core for core in (1, 0)]
     edge_row = jnp.where(top, 1, 0)
     staged = [
         pltpu.make_async_copy(
@@ -372,8 +373,11 @@
     def begin_last(n, to):
         exchange(to, 1 - edge_row, tail + n, 1, second_recv.at[groups - 1 + n]).start()
 
+    for n in range(GROUP - 2):
+        for to in other:
+            begin_last(n, to)
     for to in other:
-        for n in range(GROUP):
+        for n in range(GROUP - 2, GROUP):
             begin_last(n, to)
 
     arrived(lower.at[:, 0, cut], low_recv)
@@ -540,11 +544,16 @@
     which = lax.broadcasted_iota(jnp.int32, (per, per), 0)
     own = jnp.where(lane == which, norms[...][None, :], 0.0)
     inverse = 1.0 / jnp.sum(own, axis=1, keepdims=True)
-    copies = []
+    copies, begun = [], 0
     for s in range(per):
         held[s] = defect[s] * inverse[s : s + 1]
-        copies.append(pltpu.make_async_copy(held.at[s], out.at[s], sem.at[s]))
-        copies[-1].start()
+        if s in STOPS:
+            span = pl.ds(begun, s + 1 - begun)
+            copies.append(
+                pltpu.make_async_copy(held.at[span], out.at[span], sem.at[len(copies)])
+            )
+            copies[-1].start()
+            begun = s + 1
     for copy in copies:
         copy.wait()
 
@@ -609,7 +618,7 @@
         out_shape=block,
         in_specs=[held, held],
         out_specs=anywhere,
-        scratch_shapes=[vmem(block.shape, F32), dma((per,))],
+        scratch_shapes=[vmem(block.shape, F32), dma((len(STOPS),))],
         compiler_params=pltpu.CompilerParams(vmem_limit_bytes=16 << 20),
         cost_estimate=pl.CostEstimate(
             flops=4_000_000, bytes_accessed=8_400_000, transcendentals=0

time: 71 us -> 70.8 us (level); the launches traced: 70.9 us -> 70 us
  Pallas kernels: 70.3 us -> 69.3 us
    pallas_call x1, Pallas kernels: 68 us -> 67.1 us  [on_device(): pl.pallas_call(functools.partial(kernel, peers, amplitude), name='defect'...]
where the time goes in v5:
time: 70.8 us; the launch traced here: 70 us
  Pallas kernels  69.3 us (98%)
    pallas_call x1, Pallas kernels, on_device(): pl.pallas_call(functools.partial(kernel, peers, amplitude), name='defect'...  67.1 us
    pallas_call x1, Pallas kernels, on_device(): pl.pallas_call(scale, name='scale', out_shape=block, in_specs=[held, held...  2.2 us

profile of v5, /device:TPU:1, one launch (start us, length us, event | category | flops | bytes accessed | tf_op | source)
XLA Modules:
  0.0 70.0 jit_solution(6255685144758615802)
XLA Ops:
  0.6 67.1 %defect.1 = (f32[16,8,8192]{2,1,0:T(8,128)S(1)}, f32[1,128]{1,0:T(1,128)S(1)}) custom-call(f32[64,2,8192]{2,1,0:T(2,128)} %heat.1, f32[4,8,8192]{2,1,0:T(8,128)} %cot_hbm.1, s32[64]{0:T(128)} %sources_hbm.1), custom_call_target="tpu_custom_call" | custom-call | flops 200000000 | bytes 16000000 | tf_op jit(solution)/shard_map/defect/pallas_call | solution.py:571
  67.8 0.0 copy-start
  67.8 2.2 %scale.1 = f32[16,8,8192]{2,1,0:T(8,128)} custom-call(f32[16,8,8192]{2,1,0:T(8,128)S(1)} %get-tuple-element.4.defect, f32[16]{0:T(128)S(1)} %slice_bitcast_fusion.norms), custom_call_target="tpu_custom_call" | custom-call | flops 4000000 | bytes 8400000 | tf_op jit(solution)/shard_map/scale/pallas_call | solution.py:615
  70.0 0.0 copy-done
  (1 shorter events, 0.0 us)
Async XLA Ops:
  67.8 2.2 %copy-start = (f32[16]{0:T(128)}, f32[16]{0:T(128)S(1)}, u32[]{:S(2)}) copy-start(f32[16]{0:T(128)S(1)} %slice_bitcast_fusion.norms) | copy-start | bytes 196

commit v6 on v5

--- a/solution.py
+++ b/solution.py
@@ -194,16 +194,6 @@
     ]
     for copy in staged:
         copy.start()
-    cot_copy = pltpu.make_async_copy(cot_hbm, cot, cot_sem)
-    cot_copy.start()
-    src_copy = pltpu.make_async_copy(sources_hbm, sources, src_sem)
-    src_copy.start()
-    own = pltpu.make_async_copy(
-        heat.at[pl.ds(per * k, per)],
-        field.at[:, pl.ds(pl.multiple_of(2 * k, 2), 2)],
-        own_sem,
-    )
-    own.start()
     pl.semaphore_wait(barrier, len(near))
 
     def some(start, count):
@@ -234,6 +224,17 @@
             first_recv.at[0],
             at(v, to),
         ).start()
+
+    cot_copy = pltpu.make_async_copy(cot_hbm, cot, cot_sem)
+    cot_copy.start()
+    src_copy = pltpu.make_async_copy(sources_hbm, sources, src_sem)
+    src_copy.start()
+    own = pltpu.make_async_copy(
+        heat.at[pl.ds(per * k, per)],
+        field.at[:, pl.ds(pl.multiple_of(2 * k, 2), 2)],
+        own_sem,
+    )
+    own.start()
 
     above_side = last & (k >= 2)
     below_side = first & (k < 2)
@@ -495,13 +496,14 @@
     sums = lax.fori_loop(0, groups, group, jnp.zeros((1, LANES), F32))
 
     row[...] = sums
+    rows[0:1] = sums
 
     def tell(n, _):
         far = peers // 2 + PLANE - 1
         for step in range(TELL):
             i_step = 1 + lax.rem(far + peers - 2 - TELL * n - step, peers - 1)
             remote(
-                row, rows.at[i_step], sum_send, sum_recv, at(lax.rem(v + i_step, peers), k)
+                row, rows.at[pl.ds(i_step, 1)], sum_send, sum_recv, at(lax.rem(v + i_step, peers), k)
             ).start()
         return 0
 
@@ -533,7 +535,7 @@
         arrived(relay.at[1], relay_send.at[1])
 
     arrived(rows.at[1:peers], sum_recv)
-    sums = sums + jnp.sum(rows[1:peers], axis=0)
+    sums = jnp.sum(rows[...], axis=0, keepdims=True)
     norms[...] = jnp.sqrt(sums / (peers * 8 * width) + 1e-06)
     arrived(rows.at[1:peers], sum_send)
 
@@ -582,7 +584,7 @@
             vmem((7, rows_dev, width), F32),
             vmem((2, slots, PIECE, width), F32),
             vmem((1, LANES), F32),
-            vmem((peers, 1, LANES), F32),
+            vmem((peers, LANES), F32),
             vmem((per, width), F32),
             vmem((2, GROUP, width), F32),
             pltpu.SemaphoreType.REGULAR((6,)),

time: 70.8 us -> 70.8 us (level)
  no operation moved by 1% of the time
where the time goes in v6:
time: 70.8 us; the launch traced here: 69.9 us
  Pallas kernels  69.3 us (98%)
    pallas_call x1, Pallas kernels, on_device(): pl.pallas_call(functools.partial(kernel, peers, amplitude), name='defect'...  67.1 us
    pallas_call x1, Pallas kernels, on_device(): pl.pallas_call(scale, name='scale', out_shape=block, in_specs=[held, held...  2.2 us

profile of v6, /device:TPU:1, one launch (start us, length us, event | category | flops | bytes accessed | tf_op | source)
XLA Modules:
  0.0 69.9 jit_solution(9304949462164793469)
XLA Ops:
  0.6 67.1 %defect.1 = (f32[16,8,8192]{2,1,0:T(8,128)S(1)}, f32[1,128]{1,0:T(1,128)S(1)}) custom-call(f32[64,2,8192]{2,1,0:T(2,128)} %heat.1, f32[4,8,8192]{2,1,0:T(8,128)} %cot_hbm.1, s32[64]{0:T(128)} %sources_hbm.1), custom_call_target="tpu_custom_call" | custom-call | flops 200000000 | bytes 16000000 | tf_op jit(solution)/shard_map/defect/pallas_call | solution.py:573
  67.7 0.0 copy-start
  67.7 2.2 %scale.1 = f32[16,8,8192]{2,1,0:T(8,128)} custom-call(f32[16,8,8192]{2,1,0:T(8,128)S(1)} %get-tuple-element.4.defect, f32[16]{0:T(128)S(1)} %slice_bitcast_fusion.norms), custom_call_target="tpu_custom_call" | custom-call | flops 4000000 | bytes 8400000 | tf_op jit(solution)/shard_map/scale/pallas_call | solution.py:617
  69.9 0.0 copy-done
  (1 shorter events, 0.0 us)
Async XLA Ops:
  67.7 2.2 %copy-start = (f32[16]{0:T(128)}, f32[16]{0:T(128)S(1)}, u32[]{:S(2)}) copy-start(f32[16]{0:T(128)S(1)} %slice_bitcast_fusion.norms) | copy-start | bytes 196
